TPU v7x, 32 devices: a whole 2x2x4 slice. The times are simulated.
32 devices in a mesh: gx: 4 (over z), gy: 8 (over y, x, core).
Axes of the slice: x: 2, y: 2, z: 4, core: 2. Of those that a mesh axis runs over, the one named last changes fastest.
Arguments:
- coordinates: float32 [3, 65536], P(None, ('gx', 'gy')), may hold values from 0 to 1
- rhs: float32 [16, 65536], P(None, ('gx', 'gy')), may hold values from -70 to 70
- leaf_order: int32 [32, 2048], P(('gx', 'gy')), may hold values from 0 to 2047, each once within a row
- leaf_sizes: int32 [32], P(('gx', 'gy')), may hold values from 1 to 2048, 49152 in all
- inverse_scales: float32 [3], replicated, may hold values from 12 to 30
- noise_var: float32 [1], replicated, may hold values from 0.3 to 1
- u_factors: float32 [5, 64, 65536], P(None, None, ('gx', 'gy')), may hold values from -0.375 to 0.375
- v_factors: float32 [5, 64, 65536], P(None, None, ('gx', 'gy')), may hold values from -1 to 1
Outputs:
- solution: float32 [16, 65536], P(None, ('gx', 'gy'))
Inputs may be any that keep to these rules, and one draw needn't show every extreme that they name: `leaf_sizes`: each leaf's live points stand first in leaf order.
All inputs are finite; a program needn't handle non-finite values. No bound on the sum of `leaf_sizes` on one device may be relied on, other than what follows from the above.
Results may differ from a plain program's by a relative error of at most 0.0001.
Values sent between devices are 32-bit elements; how exact they have to be, the bound alone decides.
A program may use at most 128 MiB of HBM per device.

v0:
```python
import functools
import math

import jax
import jax.numpy as jnp
from jax import lax
from jax.experimental import pallas as pl
from jax.experimental.pallas import tpu as pltpu
from jax.sharding import PartitionSpec as P

ITERS = 3

epsilon = 1e-06
sqrt_three = math.sqrt(3.0)
log2_e = math.log2(math.e)
MESH = pl.DeviceIdType.MESH
f32 = jnp.float32
bf16 = jnp.bfloat16
NN = (((1,), (0,)), ((), ()))
NT = (((1,), (1,)), ((), ()))


def least_squares(columns, beta):
    count_cols = len(columns)
    cosines = []
    sines = []
    target = [beta] + [jnp.zeros_like(beta)] * count_cols
    upper = []
    for column_idx in range(count_cols):
        entries = list(columns[column_idx])
        for row_idx in range(column_idx):
            first_val = entries[row_idx]
            second_val = entries[row_idx + 1]
            entries[row_idx] = cosines[row_idx] * first_val + sines[row_idx] * second_val
            entries[row_idx + 1] = -sines[row_idx] * first_val + cosines[row_idx] * second_val
        first_val = entries[column_idx]
        second_val = entries[column_idx + 1]
        radius = jnp.sqrt(first_val * first_val + second_val * second_val)
        cosines.append(first_val / radius)
        sines.append(second_val / radius)
        entries[column_idx] = radius
        carried = target[column_idx]
        target[column_idx] = cosines[column_idx] * carried
        target[column_idx + 1] = -sines[column_idx] * carried
        upper.append(entries[: column_idx + 1])
    weights = [None] * count_cols
    for column_idx in reversed(range(count_cols)):
        accum = target[column_idx]
        for later_idx in range(column_idx + 1, count_cols):
            accum = accum - upper[later_idx][column_idx] * weights[later_idx]
        weights[column_idx] = accum / upper[column_idx][column_idx]
    return weights


def flipped(index, bits):
    result = index
    place = 1
    while place <= bits:
        if bits & place:
            result = result + place * (1 - 2 * lax.rem(lax.div(index, place), 2))
        place *= 2
    return result


def split2(value):
    high = value.astype(bf16)
    low = (value - high.astype(f32)).astype(bf16)
    return high, low


def split3(value):
    high = value.astype(bf16)
    rest = value - high.astype(f32)
    mid = rest.astype(bf16)
    low = (rest - mid.astype(f32)).astype(bf16)
    return high, mid, low


def dot(left, right, dims=NN):
    return lax.dot_general(left, right, dims, preferred_element_type=f32)


def fused(
    size_gx, size_gy,
    coords_ref, rhs_ref, order_ref, sizes_ref, inv_ref, noise_ref, u_hbm, v_hbm,
    out_ref,
    near_hi, near_lo, columns_pos, rows_pos, u_raw, v_raw, u_hi, u_lo, v_hi, v_lo,
    basis_ref, image_ref,
    send_part, recv_low, recv_high, send_node, recv_node,
    send_dots, recv_dots,
    load_sem,
    part_s, part_r, node_s, node_r, dots_s, dots_r,
):
    me_x = lax.axis_index("gx")
    me_y = lax.axis_index("gy")
    levels_low = size_gy.bit_length() - 1
    levels_high = size_gx.bit_length() - 1
    nv, leaf_len = rhs_ref.shape
    num_dims = coords_ref.shape[0]
    num_levels, num_rank = u_raw.shape[0], u_raw.shape[1]
    half = nv // 2
    lanes = 2 * num_rank
    size_all = size_gx * size_gy

    u_load = pltpu.make_async_copy(u_hbm, u_raw, load_sem.at[0])
    v_load = pltpu.make_async_copy(v_hbm, v_raw, load_sem.at[1])
    v_load.start()
    u_load.start()

    peers = [
        (flipped(me_x, apart // size_gy), flipped(me_y, apart % size_gy)) for apart in range(size_all)
    ]
    barrier = pltpu.get_barrier_semaphore()
    for apart in range(1, size_all):
        pl.semaphore_signal(barrier, inc=1, device_id=peers[apart], device_id_type=MESH)

    def send(src, dst, sems, semr, device):
        copy = pltpu.make_async_remote_copy(
            src_ref=src, dst_ref=dst, send_sem=sems, recv_sem=semr,
            device_id=device, device_id_type=MESH,
        )
        copy.start()
        return copy

    live = jnp.where(
        lax.broadcasted_iota(jnp.int32, (1, leaf_len), 1) < sizes_ref[0], 1.0, 0.0
    ).astype(f32)

    width = 128
    groups = leaf_len // width
    order = order_ref[...]
    outer = lax.div(order, width)
    inner = order - outer * width
    pick = jnp.where(
        lax.broadcasted_iota(jnp.int32, (width, leaf_len), 0) == inner, 1.0, 0.0
    ).astype(bf16)

    def gather(value):
        rows = value.shape[0]
        parts = []
        for part in split3(value):
            parts += [part[:, g * width : (g + 1) * width] for g in range(groups)]
        stacked = jnp.concatenate(parts, axis=0)
        pieces = []
        for start_col in range(0, leaf_len, 512):
            cols = slice(start_col, start_col + 512)
            got = dot(stacked, pick[:, cols])
            total = jnp.zeros((rows, 512), f32)
            for g in range(groups):
                terms = [
                    got[(part * groups + g) * rows : (part * groups + g + 1) * rows] for part in range(3)
                ]
                total = jnp.where(outer[:, cols] == g, terms[0] + terms[1] + terms[2], total)
            pieces.append(total)
        return jnp.concatenate(pieces, axis=1)

    pad = jnp.zeros((16 - num_dims, leaf_len), f32)
    row_sel = lax.broadcasted_iota(jnp.int32, (16, 1), 0)
    scale = jnp.zeros((16, 1), f32)
    for dim in range(num_dims):
        scale = jnp.where(row_sel == dim, inv_ref[dim], scale)
    gathered = gather(jnp.concatenate([coords_ref[...], pad], axis=0))
    rows_pos[0:16, :] = gathered * scale * sqrt_three
    rows_pos[16:, :] = jnp.zeros((rows_pos.shape[0] - 16, leaf_len), f32)
    columns_pos[...] = rows_pos[...].T
    basis_ref[0] = live * gather(rhs_ref[...])

    padded = v_hi.shape[0]
    used = num_levels * num_rank

    def prepare(raw, hi, lo):
        for level in range(num_levels):
            first, second = split2(raw[level])
            hi[level * num_rank : (level + 1) * num_rank, :] = first
            lo[level * num_rank : (level + 1) * num_rank, :] = second
        if padded > used:
            hi[used:, :] = jnp.zeros((padded - used, leaf_len), bf16)
            lo[used:, :] = jnp.zeros((padded - used, leaf_len), bf16)

    lane = lax.broadcasted_iota(jnp.int32, (half, lanes), 1)
    left_side = lane < num_rank

    def swap(value):
        return pltpu.roll(value, num_rank, 1)

    def send_partials(it, coef):
        for level in range(num_levels):
            block = coef[:, (level // 2) * lanes : (level // 2 + 1) * lanes]
            top, bottom = block[:half], block[half:]
            if level % 2 == 0:
                tile = jnp.where(left_side, top, swap(bottom))
            else:
                tile = jnp.where(left_side, swap(top), bottom)
            send_part[it, level] = tile
        copies = []
        for apart in range(1, size_gy):
            copies.append(send(
                send_part.at[it, pl.ds(levels_low, levels_high)], recv_high.at[it, apart],
                part_s.at[it, apart, 1], part_r.at[it, apart, 1], peers[apart],
            ))
        late = []
        for apart in range(1, size_gy):
            late.append(send(
                send_part.at[it, apart.bit_length() - 1], recv_low.at[it, apart],
                part_s.at[it, apart, 0], part_r.at[it, apart, 0], peers[apart],
            ))
        return copies, late

    def send_nodes(it, part_copies):
        for copy in part_copies:
            copy.wait_recv()
        total = send_part[it, levels_low:num_levels]
        for apart in range(1, size_gy):
            total = total + recv_high[it, apart]
        send_node[it] = total
        return [
            send(
                send_node.at[it, apart.bit_length() - 1], recv_node.at[it, apart],
                node_s.at[it, apart], node_r.at[it, apart], peers[apart * size_gy],
            )
            for apart in range(1, size_gx)
        ]

    def siblings(it, copies):
        for copy in copies:
            copy.wait_recv()
        tiles = []
        for count, source in ((levels_low, recv_low), (levels_high, recv_node)):
            for level in range(count):
                total = source[it, 2**level]
                for apart in range(2**level + 1, 2 ** (level + 1)):
                    total = total + source[it, apart]
                tiles.append(total)
        if len(tiles) % 2:
            tiles.append(jnp.zeros_like(tiles[0]))
        blocks = []
        for pair in range(len(tiles) // 2):
            even, odd = tiles[2 * pair], tiles[2 * pair + 1]
            top = jnp.where(left_side, even, swap(odd))
            bottom = jnp.where(left_side, swap(even), odd)
            blocks.append(jnp.concatenate([top, bottom], axis=0))
        return jnp.concatenate(blocks, axis=1)

    slots = lanes // nv
    row16 = lax.broadcasted_iota(jnp.int32, (nv, lanes), 0)
    slot16 = lax.broadcasted_iota(jnp.int32, (nv, lanes), 1) - row16 * slots

    def send_sums(it, values):
        block = jnp.zeros((nv, lanes), f32)
        for idx, value in enumerate(values):
            block = jnp.where(slot16 == idx, value, block)
        send_dots[it] = jnp.sum(block, axis=0, keepdims=True)
        return [
            send(
                send_dots.at[it], recv_dots.at[it, apart],
                dots_s.at[it, apart], dots_r.at[it, apart], peers[apart],
            )
            for apart in range(1, size_all)
        ]

    def read_sums(it, copies, count):
        for copy in copies:
            copy.wait_recv()
        terms = [send_dots[it]] + [recv_dots[it, apart] for apart in range(1, size_all)]
        while len(terms) > 1:
            terms = [terms[i] + terms[i + 1] for i in range(0, len(terms), 2)]
        return [
            jnp.sum(jnp.where(slot16 == idx, terms[0], 0.0), axis=1, keepdims=True)
            for idx in range(count)
        ]

    chunk = min(512, leaf_len)

    def near_columns(both, first, begin, end):
        for low in range(begin, end, chunk):
            high = low + chunk
            cols = slice(low, high)
            wide = dot(both[:, :high], near_hi[:high, cols])
            rest = dot(first[:, :high], near_lo[:high, cols])
            if high < leaf_len:
                wide = wide + dot(both[:, high:], near_hi[cols, high:], NT)
                rest = rest + dot(first[:, high:], near_lo[cols, high:], NT)
            image_ref[:, cols] = wide[:nv] + wide[nv:] + rest

    rows = 16

    def fill_near():
        for low in range(0, leaf_len, chunk):
            cols = slice(low, low + chunk)

            def fill(block, carry, cols=cols):
                base = pl.multiple_of(block * rows, rows)
                square = None
                for dim in range(num_dims):
                    differ = columns_pos[pl.ds(base, rows), dim : dim + 1] - rows_pos[dim : dim + 1, cols]
                    square = differ * differ if square is None else square + differ * differ
                distance = square * lax.rsqrt(jnp.maximum(square, 1e-30))
                value = (1.0 + distance) * jnp.exp2(distance * (-log2_e))
                hi, lo = split2(value)
                near_hi[pl.ds(base, rows), cols] = hi
                near_lo[pl.ds(base, rows), cols] = lo
                return carry

            lax.fori_loop(0, (low + chunk) // rows, fill, 0, unroll=4)

    pending = []

    def operate(it, vector):
        first, second = split2(vector)
        both = jnp.concatenate([first, second], axis=0)
        if it == 0:
            v_load.wait()
            prepare(v_raw, v_hi, v_lo)
        wide = dot(both, v_hi[...], NT)
        coef = wide[:nv] + wide[nv:] + dot(first, v_lo[...], NT)
        if it == 0:
            pl.semaphore_wait(barrier, size_all - 1)
        parts, late = send_partials(it, coef)
        if it == 0:
            fill_near()
            u_load.wait()
            prepare(u_raw, u_hi, u_lo)
            nodes = send_nodes(it, parts)
            near_columns(both, first, 0, leaf_len)
        else:
            near_columns(both, first, 0, leaf_len // 2)
            nodes = send_nodes(it, parts)
            near_columns(both, first, leaf_len // 2, leaf_len)
        coef_hi, coef_lo = split2(siblings(it, late + nodes))
        wide = dot(jnp.concatenate([coef_hi, coef_lo], axis=0), u_hi[...])
        far = wide[:nv] + wide[nv:] + dot(coef_hi, u_lo[...])
        pending.extend(parts + late + nodes)
        return live * (image_ref[...] + far) - vector

    def lane_sum(value):
        return jnp.sum(value, axis=1, keepdims=True)

    shift = 1.0 + noise_ref[0]
    gram = {}
    columns = []
    images = []
    beta = None
    raw = basis_ref[0]
    image = operate(0, raw)
    for it in range(ITERS):
        last = it + 1 == ITERS
        values = [lane_sum(basis_ref[row] * image) for row in range(it)] + [lane_sum(raw * image)]
        values += [lane_sum(basis_ref[row] * raw) for row in range(it)] + [lane_sum(raw * raw)]
        if last:
            values.append(lane_sum(image * image))
        copies = send_sums(it, values)
        pending.extend(copies)
        ahead = None if last else operate(it + 1, image)
        sums = read_sums(it, copies, len(values))
        length = jnp.sqrt(sums[2 * it + 1] + epsilon)
        inverse = 1.0 / length
        if it == 0:
            beta = length
        else:
            columns[-1].append(length)
        products = [value * inverse for value in sums[: it + 1]]
        products[it] = products[it] * inverse
        lengths = [value * inverse for value in sums[it + 1 : 2 * it + 2]]
        lengths[it] = lengths[it] * inverse
        vector = raw * inverse
        basis_ref[it] = vector
        for row in range(it + 1):
            gram[row, it] = gram[it, row] = lengths[row]
        column = [products[row] + shift * lengths[row] for row in range(it + 1)]
        moved = [column[row] - shift if row == it else column[row] for row in range(it + 1)]
        columns.append(list(column))
        if last:
            rest = sums[-1] * inverse * inverse
            for row in range(it + 1):
                inside = -2.0 * products[row]
                for other in range(it + 1):
                    inside = inside + moved[other] * gram[row, other]
                rest = rest + moved[row] * inside
            columns[-1].append(jnp.sqrt(jnp.maximum(rest, 0.0) + epsilon))
        else:
            images.append(image * inverse)
            raw = images[it]
            image = ahead * inverse
            for row in range(it + 1):
                raw = raw - moved[row] * basis_ref[row]
                image = image - moved[row] * images[row]
    weights = least_squares(columns, beta)
    solved = weights[0] * basis_ref[0]
    for it in range(1, ITERS):
        solved = solved + weights[it] * basis_ref[it]
    parts = split3(solved)
    for g in range(groups):
        mask = jnp.where(outer == g, 1.0, 0.0).astype(bf16)
        stacked = jnp.concatenate([part * mask for part in parts], axis=0)
        got = dot(stacked, pick, NT)
        out_ref[:, g * width : (g + 1) * width] = got[:nv] + got[nv : 2 * nv] + got[2 * nv :]
    for copy in pending:
        copy.wait_send()


def per_device(
    size_gx, size_gy,
    coordinates, rhs, leaf_order, leaf_sizes, inverse_scales, noise_var, u_factors, v_factors,
):
    num_vectors, leaf_len = rhs.shape
    num_levels, num_rank = u_factors.shape[0], u_factors.shape[1]
    levels_high = size_gx.bit_length() - 1
    half, lanes = num_vectors // 2, 2 * num_rank
    padded = (num_levels + 1) // 2 * 2 * num_rank
    tile = (half, lanes)
    vmem = pl.BlockSpec(memory_space=pltpu.VMEM)
    smem = pl.BlockSpec(memory_space=pltpu.SMEM)
    any_space = pl.BlockSpec(memory_space=pl.ANY)
    dma = pltpu.SemaphoreType.DMA
    return pl.pallas_call(
        functools.partial(fused, size_gx, size_gy),
        out_shape=jax.ShapeDtypeStruct(rhs.shape, f32),
        in_specs=[vmem, vmem, vmem, smem, smem, smem, any_space, any_space],
        out_specs=vmem,
        scratch_shapes=[
            pltpu.VMEM((leaf_len, leaf_len), bf16),
            pltpu.VMEM((leaf_len, leaf_len), bf16),
            pltpu.VMEM((leaf_len, 128), f32),
            pltpu.VMEM((128, leaf_len), f32),
            pltpu.VMEM(u_factors.shape, f32),
            pltpu.VMEM(v_factors.shape, f32),
            pltpu.VMEM((padded, leaf_len), bf16),
            pltpu.VMEM((padded, leaf_len), bf16),
            pltpu.VMEM((padded, leaf_len), bf16),
            pltpu.VMEM((padded, leaf_len), bf16),
            pltpu.VMEM((ITERS,) + rhs.shape, f32),
            pltpu.VMEM(rhs.shape, f32),
            pltpu.VMEM((ITERS, num_levels) + tile, f32),
            pltpu.VMEM((ITERS, size_gy) + tile, f32),
            pltpu.VMEM((ITERS, size_gy, levels_high) + tile, f32),
            pltpu.VMEM((ITERS, levels_high) + tile, f32),
            pltpu.VMEM((ITERS, size_gx) + tile, f32),
            pltpu.VMEM((ITERS, 1, lanes), f32),
            pltpu.VMEM((ITERS, size_gx * size_gy, 1, lanes), f32),
            dma((2,)),
            dma((ITERS, size_gy, 2)),
            dma((ITERS, size_gy, 2)),
            dma((ITERS, size_gx)),
            dma((ITERS, size_gx)),
            dma((ITERS, size_gx * size_gy)),
            dma((ITERS, size_gx * size_gy)),
        ],
        compiler_params=pltpu.CompilerParams(collective_id=0, has_side_effects=True),
        name="gmres",
    )(coordinates, rhs, leaf_order, leaf_sizes, inverse_scales, noise_var, u_factors, v_factors)


def solution(mesh):
    in_specs = (
        P(None, ("gx", "gy")),
        P(None, ("gx", "gy")),
        P(("gx", "gy"), None),
        P(("gx", "gy")),
        P(),
        P(),
        P(None, None, ("gx", "gy")),
        P(None, None, ("gx", "gy")),
    )
    out_specs = P(None, ("gx", "gy"))
    return jax.shard_map(
        functools.partial(per_device, mesh.shape["gx"], mesh.shape["gy"]),
        mesh=mesh, in_specs=in_specs, out_specs=out_specs, check_vma=False,
    )
```

profile of v0, /device:TPU:0, one launch (start us, length us, event | category | flops | bytes accessed | tf_op | source)
XLA Modules:
  0.0 57.8 jit_solution(7343250783903482979)
XLA Ops:
  1.3 54.9 %gmres.1 = f32[16,2048]{1,0:T(8,128)} custom-call(f32[3,2048]{1,0:T(4,128)} %coords_ref.1, f32[16,2048]{1,0:T(8,128)} %rhs_ref.1, s32[1,2048]{1,0:T(1,128)} %order_ref.1, s32[1]{0:T(128)S(6)} %copy.10.sizes_ref, f32[3]{0:T(128)} %inv_ref.1, f32[1]{0:T(128)S(6)} %copy.11.noise_ref, f32[5,64,2048]{2,1,0:T(8,128)} %u_hbm.1, f32[5,64,2048]{2,1,0:T(8,128)} %v_hbm.1), custom_call_target="tpu_custom_call" | custom-call | tf_op jit(solution)/shard_map/gmres/pallas_call | solution.py:415
  56.2 1.6 %copy.12 = f32[16,2048]{1,0:T(8,128)} copy(f32[16,2048]{1,0:T(8,128)} %gmres.1) | data formatting | bytes 262144
where the time goes:
time: 58 us; the launch traced here: 57.8 us
  Pallas kernels  54.9 us (95%)
  local copies, waits for them, and re-layouts  1.57 us (3%)
  between operations  1.31 us (2%)
    pallas_call x1, Pallas kernels, per_device(): pl.pallas_call(functools.partial(fused, size_gx, size_gy), out_shape=jax....  54.9 us
    unnamed x1, local copies, waits for them, and re-layouts  1.57 us

commit v1 on v0

--- a/solution.py
+++ b/solution.py
@@ -284,8 +284,8 @@
 
     rows = 16
 
-    def fill_near():
-        for low in range(0, leaf_len, chunk):
+    def fill_near(begin, end):
+        for low in range(begin, end, chunk):
             cols = slice(low, low + chunk)
 
             def fill(block, carry, cols=cols):
@@ -301,7 +301,7 @@
                 near_lo[pl.ds(base, rows), cols] = lo
                 return carry
 
-            lax.fori_loop(0, (low + chunk) // rows, fill, 0, unroll=4)
+            lax.fori_loop(0, (low + chunk) // rows, fill, 0, unroll=16)
 
     pending = []
 
@@ -317,10 +317,11 @@
             pl.semaphore_wait(barrier, size_all - 1)
         parts, late = send_partials(it, coef)
         if it == 0:
-            fill_near()
+            fill_near(0, leaf_len - chunk)
+            nodes = send_nodes(it, parts)
+            fill_near(leaf_len - chunk, leaf_len)
             u_load.wait()
             prepare(u_raw, u_hi, u_lo)
-            nodes = send_nodes(it, parts)
             near_columns(both, first, 0, leaf_len)
         else:
             near_columns(both, first, 0, leaf_len // 2)
@@ -349,8 +350,14 @@
         if last:
             values.append(lane_sum(image * image))
         copies = send_sums(it, values)
+        if last:
+            for copy in pending:
+                copy.wait_send()
+            pending = []
+            ahead = None
+        else:
+            ahead = operate(it + 1, image)
         pending.extend(copies)
-        ahead = None if last else operate(it + 1, image)
         sums = read_sums(it, copies, len(values))
         length = jnp.sqrt(sums[2 * it + 1] + epsilon)
         inverse = 1.0 / length

time: 58 us -> 53.1 us (0.916)
  Pallas kernels: 54.9 us -> 50.1 us
    pallas_call x1, Pallas kernels: 54.9 us -> 50.1 us  [per_device(): pl.pallas_call(functools.partial(fused, size_gx, size_gy), out_shape=jax....]
where the time goes in v1:
time: 53.1 us; the launch traced here: 53 us
  Pallas kernels  50.1 us (94%)
  local copies, waits for them, and re-layouts  1.57 us (3%)
  between operations  1.31 us (2%)
    pallas_call x1, Pallas kernels, per_device(): pl.pallas_call(functools.partial(fused, size_gx, size_gy), out_shape=jax....  50.1 us
    unnamed x1, local copies, waits for them, and re-layouts  1.57 us

profile of v1, /device:TPU:0, one launch (start us, length us, event | category | flops | bytes accessed | tf_op | source)
XLA Modules:
  0.0 53.0 jit_solution(13185891897047487705)
XLA Ops:
  1.3 50.1 %gmres.1 = f32[16,2048]{1,0:T(8,128)} custom-call(f32[3,2048]{1,0:T(4,128)} %coords_ref.1, f32[16,2048]{1,0:T(8,128)} %rhs_ref.1, s32[1,2048]{1,0:T(1,128)} %order_ref.1, s32[1]{0:T(128)S(6)} %copy.10.sizes_ref, f32[3]{0:T(128)} %inv_ref.1, f32[1]{0:T(128)S(6)} %copy.11.noise_ref, f32[5,64,2048]{2,1,0:T(8,128)} %u_hbm.1, f32[5,64,2048]{2,1,0:T(8,128)} %v_hbm.1), custom_call_target="tpu_custom_call" | custom-call | tf_op jit(solution)/shard_map/gmres/pallas_call | solution.py:422
  51.4 1.6 %copy.12 = f32[16,2048]{1,0:T(8,128)} copy(f32[16,2048]{1,0:T(8,128)} %gmres.1) | data formatting | bytes 262144
